TPU v7x, 32 devices: a whole 2x2x4 slice. The times are simulated.
32 devices in a mesh: row: 8 (over z, x), col: 4 (over y, core).
Axes of the slice: x: 2, y: 2, z: 4, core: 2. Of those that a mesh axis runs over, the one named last changes fastest.
Arguments:
- voltage: float32 [2, 4096, 16384], P(None, ('row', 'col')), may hold values from -6 to 6
- chirp_phase: float32 [16384, 4096], P(('row', 'col')), may hold values from -3.140625 to 3.140625
- filter_taps: float32 [8, 1024], replicated, may hold values from -0.0625 to 0.0625
Outputs:
- filterbank: float32 [2, 1024, 65536], P(None, None, ('row', 'col'))
All inputs are finite; a program needn't handle non-finite values.
Results may differ from a plain program's by a relative error of at most 0.00015.
Values sent between devices are 32-bit elements; how exact they have to be, the bound alone decides.
No kernel may reach another device: no remote copies, remote signals or barrier semaphores. Data moves between devices by JAX's collectives and lax.ppermute only.
A program may use at most 192 MiB of HBM per device.

v0:
```python
import math
import jax
import jax.numpy as jnp
from jax import lax
from jax.sharding import PartitionSpec as P

precise = lax.Precision.HIGHEST


def passed_along(block, axis, distance):
    devices = range(lax.axis_size(axis))
    route = [(i - distance, i) for i in devices if i - distance in devices]
    return lax.ppermute(block, axis, route)


def dft_table(radix, direction):
    digits = jnp.arange(radix, dtype=jnp.int32)
    product = digits[:, None] * digits[None, :] % radix
    turn = direction * 2.0 * math.pi / radix * product.astype(jnp.float32)
    cos_part = jnp.cos(turn)
    sin_part = jnp.sin(turn)
    upper = jnp.stack([cos_part, sin_part], axis=1)
    lower = jnp.stack([-sin_part, cos_part], axis=1)
    return jnp.stack([upper, lower], axis=0)


def complex_product(values, cos_part, sin_part):
    real_part = values[0] * cos_part - values[1] * sin_part
    imag_part = values[0] * sin_part + values[1] * cos_part
    return jnp.stack([real_part, imag_part])


def inner_twist(outer_radix, inner_radix, direction):
    outer_digits = jnp.arange(outer_radix, dtype=jnp.int32)
    inner_digits = jnp.arange(inner_radix, dtype=jnp.int32)
    length = outer_radix * inner_radix
    product = outer_digits[:, None] * inner_digits[None, :] % length
    turn = direction * 2.0 * math.pi / length * product.astype(jnp.float32)
    return (jnp.cos(turn), jnp.sin(turn))


def dft_rows(values, direction):
    length = values.shape[1]
    column_count = values.shape[2]
    inner_radix = min(length, 128)
    outer_radix = length // inner_radix
    blocked = values.reshape(2, outer_radix, inner_radix, column_count)
    partial_value = jnp.einsum(
        "cadk,cabm->dkbm", dft_table(outer_radix, direction), blocked, precision=precise
    )
    cos_part, sin_part = inner_twist(outer_radix, inner_radix, direction)
    partial_value = complex_product(partial_value, cos_part[:, :, None], sin_part[:, :, None])
    result = jnp.einsum(
        "cbdq,ckbm->dqkm", dft_table(inner_radix, direction), partial_value, precision=precise
    )
    return result.reshape(2, length, column_count)


def dft_cols(values, direction):
    length = values.shape[2]
    row_count = values.shape[1]
    inner_radix = min(length, 128)
    outer_radix = length // inner_radix
    blocked = values.reshape(2, row_count, outer_radix, inner_radix)
    partial_value = jnp.einsum(
        "cadk,cmab->dmkb", dft_table(outer_radix, direction), blocked, precision=precise
    )
    cos_part, sin_part = inner_twist(outer_radix, inner_radix, direction)
    partial_value = complex_product(partial_value, cos_part, sin_part)
    result = jnp.einsum(
        "cbdq,cmkb->dmqk", dft_table(inner_radix, direction), partial_value, precision=precise
    )
    return result.reshape(2, row_count, length)


def rotate(values, row_index, col_index, total, direction, factor):
    product = row_index[:, None] * col_index[None, :] % total
    turn = direction * 2.0 * math.pi / total * product.astype(jnp.float32)
    return complex_product(values, factor * jnp.cos(turn), factor * jnp.sin(turn))


def spread(values):
    return lax.all_to_all(values, ("row", "col"), split_axis=2, concat_axis=1, tiled=True)


def collect(values):
    return lax.all_to_all(values, ("row", "col"), split_axis=1, concat_axis=2, tiled=True)


def local(voltage, chirp_phase, filter_taps):
    device_count = lax.axis_size("row") * lax.axis_size("col")
    device = lax.axis_index(("row", "col"))
    local_rows = voltage.shape[1]
    total_rows = local_rows * device_count
    total_cols = voltage.shape[2]
    local_cols = total_cols // device_count
    total = total_rows * total_cols
    signal = spread(voltage)
    signal = dft_rows(signal, -1.0)
    row_index = jnp.arange(total_rows, dtype=jnp.int32)
    col_index = device * local_cols + jnp.arange(local_cols, dtype=jnp.int32)
    signal = rotate(signal, row_index, col_index, total, -1.0, 1.0)
    signal = collect(signal)
    signal = dft_cols(signal, -1.0)
    turned_phase = jnp.transpose(chirp_phase)
    local_phase = lax.all_to_all(
        turned_phase, ("row", "col"), split_axis=0, concat_axis=1, tiled=True
    )
    signal = complex_product(signal, jnp.cos(local_phase), jnp.sin(local_phase))
    signal = dft_cols(signal, 1.0)
    row_index = device * local_rows + jnp.arange(local_rows, dtype=jnp.int32)
    col_index = jnp.arange(total_cols, dtype=jnp.int32)
    signal = rotate(signal, row_index, col_index, total, 1.0, 1.0 / total)
    signal = spread(signal)
    signal = dft_rows(signal, 1.0)
    signal = collect(signal)
    tap_count = filter_taps.shape[0]
    channel_count = filter_taps.shape[1]
    samples = signal.reshape(2, local_rows * total_cols)
    frame_count = samples.shape[1] // channel_count
    frames = samples.reshape(2, frame_count, channel_count)
    history = passed_along(frames[:, frame_count - tap_count + 1 :, :], ("row", "col"), 1)
    extended = jnp.concatenate([history, frames], axis=1)
    turned = jnp.transpose(extended, (0, 2, 1))
    weighted = jnp.zeros((2, channel_count, frame_count), jnp.float32)
    for tap_delay in range(tap_count):
        offset = tap_count - 1 - tap_delay
        weighted = (
            weighted
            + filter_taps[tap_delay][None, :, None] * turned[:, :, offset : offset + frame_count]
        )
    return dft_rows(weighted, -1.0)


def solution(mesh):
    in_specs = (P(None, ("row", "col"), None), P(("row", "col"), None), P())
    out_specs = P(None, None, ("row", "col"))
    return jax.shard_map(local, mesh=mesh, in_specs=in_specs, out_specs=out_specs, check_vma=False)
```

profile of v0, /device:TPU:6, one launch (start us, length us, event | category | flops | bytes accessed | tf_op | source)
XLA Modules:
  0.0 2393.4 jit_solution(8709069159866349502)
XLA Ops:
  0.0 24.9 %copy.169 = f32[2,128,16384]{1,0,2:T(2,128)} copy(f32[2,128,16384]{2,1,0:T(8,128)} %param.3) | data formatting | bytes 33554432 | tf_op args[0]
  40.1 370.0 %all-to-all-done = f32[2,128,16384]{1,0,2:T(2,128)} async-done(((f32[2,128,16384]{1,0,2:T(2,128)}), f32[2,128,16384]{1,0,2:T(2,128)}, u32[]{:S(2)}, u32[]{:S(2)}) %all-to-all-start) | async-done | bytes 16777248 | tf_op jit(solution)/shard_map/all_to_all | solution.py:83
  414.6 20.2 copy.234
  434.8 21.7 fusion.71
  466.8 28.9 %fusion.59 = f32[2,128,32,512]{3,1,2,0:T(8,128)S(1)} fusion(f32[2,32,128,512]{3,1,2,0:T(8,128)S(1)} %pad_maximum_fusion, f32[1,128,2,128]{1,3,0,2:T(8,128)S(1)} %get-tuple-element.30, f32[1,128,2,128]{1,3,0,2:T(8,128)S(1)} %get-tuple-element.29), kind=kOutput, calls=%fused_computation.103 | convolution fusion | flops 12884967424 | bytes 33816576 | tf_op jit(solution)/shard_map/cbdq,ckbm->dqkm/dot_general | solution.py:53
  519.2 36.9 %fusion.51 = (f32[1,4096,512]{2,1,0:T(8,128)S(1)}, f32[1,4096,512]{2,1,0:T(8,128)S(1)}) fusion(f32[1,128,32,512]{3,2,1,0:T(8,128)S(1)} %copy.173, f32[1,128,32,512]{3,2,1,0:T(8,128)S(1)} %copy.172, s32[512]{0:T(512)S(1)} %iota_add_fusion), kind=kLoop, calls=%fused_computation.77 | loop fusion | flops 41943040 | bytes 33556480 | tf_op jit(solution)/shard_map/sub | solution.py:28
  557.9 32.2 %copy.174 = f32[2,4096,512]{2,0,1:T(2,128)} copy(f32[2,4096,512]{2,1,0:T(8,128)S(1)} %pad_maximum_fusion.1) | data formatting | bytes 33554432 | tf_op jit(solution)/shard_map/stack | solution.py:30
  607.9 31.5 %sine_bitcast_fusion = (f32[128,32,512]{2,0,1:T(8,128)}, f32[128,32,512]{2,0,1:T(8,128)}) fusion(f32[32,128,512]{2,1,0:T(8,128)} %all-to-all-done.2), kind=kLoop, calls=%fused_computation.93 | loop fusion | bytes 25165824 | tf_op jit(solution)/shard_map/sin | solution.py:109
  676.1 309.5 %all-to-all-done.1 = f32[2,4096,512]{2,0,1:T(2,128)} async-done(((f32[2,4096,512]{2,0,1:T(2,128)}), f32[2,4096,512]{2,0,1:T(2,128)}, u32[]{:S(2)}, u32[]{:S(2)}) %all-to-all-start.1) | async-done | bytes 16777248 | tf_op jit(solution)/shard_map/all_to_all | solution.py:87
  999.7 17.5 copy.176
  1017.2 18.1 copy.211
  1035.3 17.1 convolution_bitcast_fusion
  1059.4 31.5 %fusion.36 = f32[2,128,128,128]{2,3,0,1:T(8,128)} fusion(f32[1,128,128,128]{2,3,0,1:T(8,128)} %get-tuple-element.14, f32[1,128,128,128]{2,3,0,1:T(8,128)} %get-tuple-element.13, f32[1,128,2,128]{1,3,0,2:T(8,128)S(1)} %get-tuple-element.30, f32[1,128,2,128]{1,3,0,2:T(8,128)S(1)} %get-tuple-element.29), kind=kOutput, calls=%fused_computation.59 | convolution fusion | flops 12889161728 | bytes 33816576 | tf_op jit(solution)/shard_map/cbdq,cmkb->dmqk/dot_general | solution.py:70
  1090.9 19.0 multiply_subtract_fusion.3
  1109.8 17.3 fusion.37
  1134.3 31.7 %fusion.40 = f32[2,128,128,128]{2,3,0,1:T(8,128)S(1)} fusion(f32[1,128,128,128]{2,3,0,1:T(8,128)} %get-tuple-element.12, f32[1,128,128,128]{2,3,0,1:T(8,128)} %get-tuple-element.11, f32[1,128,2,128]{1,3,2,0:T(8,128)S(1)} %get-tuple-element.28, f32[1,128,2,128]{1,3,2,0:T(8,128)S(1)} %get-tuple-element.27), kind=kOutput, calls=%fused_computation.61 | convolution fusion | flops 12889161728 | bytes 33816576 | tf_op jit(solution)/shard_map/cbdq,cmkb->dmqk/dot_general | solution.py:70
  1191.5 36.6 %fusion.49 = (f32[1,128,16384]{1,2,0:T(8,128)S(1)}, f32[1,128,16384]{1,2,0:T(8,128)S(1)}) fusion(f32[1,128,128,128]{1,3,2,0:T(8,128)} %copy.192, f32[1,128,128,128]{1,3,2,0:T(8,128)} %copy.191, s32[128]{0:T(128)S(1)} %iota_add_fusion.1), kind=kLoop, calls=%fused_computation.71 | loop fusion | flops 46137344 | bytes 33554944 | tf_op jit(solution)/shard_map/sub | solution.py:28
  1229.2 61.7 %copy.193 = f32[2,128,16384]{1,0,2:T(2,128)} copy(f32[2,128,16384]{1,2,0:T(8,128)S(1)} %pad_maximum_fusion.2) | data formatting | bytes 33554432 | tf_op jit(solution)/shard_map/stack | solution.py:30
  1295.5 377.9 %all-to-all-done.3 = f32[2,128,16384]{1,0,2:T(2,128)} async-done(((f32[2,128,16384]{1,0,2:T(2,128)}), f32[2,128,16384]{1,0,2:T(2,128)}, u32[]{:S(2)}, u32[]{:S(2)}) %all-to-all-start.3) | async-done | bytes 16777248 | tf_op jit(solution)/shard_map/all_to_all | solution.py:83
  1673.4 20.1 copy.247
  1693.4 21.7 fusion.74
  1725.4 28.9 %fusion.62 = f32[2,128,32,512]{3,1,2,0:T(8,128)S(1)} fusion(f32[2,32,128,512]{3,1,2,0:T(8,128)S(1)} %pad_maximum_fusion.3, f32[1,128,2,128]{1,3,2,0:T(8,128)S(1)} %get-tuple-element.28, f32[1,128,2,128]{1,3,2,0:T(8,128)S(1)} %get-tuple-element.27), kind=kOutput, calls=%fused_computation.104 | convolution fusion | flops 12884967424 | bytes 33816576 | tf_op jit(solution)/shard_map/cbdq,ckbm->dqkm/dot_general | solution.py:53
  1754.3 20.1 copy.198
  1774.4 28.6 %copy.199 = f32[2,4096,512]{2,0,1:T(2,128)} copy(f32[2,4096,512]{2,1,0:T(8,128)} %bitcast.229) | data formatting | bytes 33554432 | tf_op jit(solution)/shard_map/reshape | solution.py:56
  1807.3 377.8 %all-to-all-done.4 = f32[2,4096,512]{2,0,1:T(2,128)} async-done(((f32[2,4096,512]{2,0,1:T(2,128)}), f32[2,4096,512]{2,0,1:T(2,128)}, u32[]{:S(2)}, u32[]{:S(2)}) %all-to-all-start.4) | async-done | bytes 16777248 | tf_op jit(solution)/shard_map/all_to_all | solution.py:87
  2185.1 17.8 copy.279
  2202.9 19.2 reshape_reshape.3
  2240.3 50.0 %fusion = f32[2,1024,2048]{1,2,0:T(8,128)} fusion(f32[2,1024,2055]{1,2,0:T(8,128)} %maximum_bitcast_fusion, f32[1024]{0:T(1024)S(1)} %bitcast.241, f32[1024]{0:T(1024)S(1)} %bitcast.242, f32[1024]{0:T(1024)S(1)} %bitcast.236, f32[1024]{0:T(1024)S(1)} %bitcast.237, f32[1024]{0:T(1024)S(1)} %bitcast.238, f32[1024]{0:T(1024)S(1)} %bitcast.239, ...), kind=kLoop, calls=%fused_computation.2 | loop fusion | flops 62914560 | bytes 151027712 | tf_op jit(solution)/shard_map/add | solution.py:129
  2290.3 17.3 copy.201
  2307.7 32.0 %fusion.65 = f32[2,8,128,2048]{3,1,2,0:T(8,128)} fusion(f32[2,8,128,2048]{3,2,1,0:T(8,128)} %bitcast.231, f32[1,8,2,8]{1,3,0,2:T(8,128)S(1)} %copy.167, f32[1,8,2,8]{1,3,0,2:T(8,128)S(1)} %copy.166), kind=kOutput, calls=%fused_computation.105 | convolution fusion | flops 805306624 | bytes 33555456 | tf_op jit(solution)/shard_map/cadk,cabm->dkbm/dot_general | solution.py:48
  2349.0 23.7 fusion.68
  2372.7 20.2 copy.278
  (70 shorter events, 210.8 us)
Async XLA Ops:
  24.9 385.2 %all-to-all-start = ((f32[2,128,16384]{1,0,2:T(2,128)}), f32[2,128,16384]{1,0,2:T(2,128)}, u32[]{:S(2)}, u32[]{:S(2)}) async-start(f32[2,128,16384]{1,0,2:T(2,128)} %copy.169), calls=%async_computation | async-start | bytes 33554432 | tf_op jit(solution)/shard_map/all_to_all | solution.py:83
  410.1 191.6 %all-to-all-start.2 = ((f32[32,128,512]{2,1,0:T(8,128)}), f32[32,128,512]{2,1,0:T(8,128)}, u32[]{:S(2)}, u32[]{:S(2)}) async-start(f32[32,128,512]{2,1,0:T(8,128)} %bitcast.232), calls=%async_computation.2 | async-start | bytes 16777216 | tf_op jit(solution)/shard_map/all_to_all | solution.py:106
  414.6 644.8 %copy-start = (f32[1,128,2,128]{1,3,0,2:T(8,128)}, f32[1,128,2,128]{1,3,0,2:T(8,128)S(1)}, u32[]{:S(2)}) copy-start(f32[1,128,2,128]{1,3,0,2:T(8,128)S(1)} %get-tuple-element.29) | copy-start | bytes 393220
  414.6 644.8 %copy-start.2 = (f32[1,128,2,128]{1,3,0,2:T(8,128)}, f32[1,128,2,128]{1,3,0,2:T(8,128)S(1)}, u32[]{:S(2)}) copy-start(f32[1,128,2,128]{1,3,0,2:T(8,128)S(1)} %get-tuple-element.30) | copy-start | bytes 393220
  601.7 383.8 %all-to-all-start.1 = ((f32[2,4096,512]{2,0,1:T(2,128)}), f32[2,4096,512]{2,0,1:T(2,128)}, u32[]{:S(2)}, u32[]{:S(2)}) async-start(f32[2,4096,512]{2,0,1:T(2,128)} %copy.174), calls=%async_computation.1 | async-start | bytes 33554432 | tf_op jit(solution)/shard_map/all_to_all | solution.py:87
  1291.0 382.4 %all-to-all-start.3 = ((f32[2,128,16384]{1,0,2:T(2,128)}), f32[2,128,16384]{1,0,2:T(2,128)}, u32[]{:S(2)}, u32[]{:S(2)}) async-start(f32[2,128,16384]{1,0,2:T(2,128)} %copy.193), calls=%async_computation.3 | async-start | bytes 33554432 | tf_op jit(solution)/shard_map/all_to_all | solution.py:83
  1803.0 4.2 copy-start.4
  1803.0 382.1 %all-to-all-start.4 = ((f32[2,4096,512]{2,0,1:T(2,128)}), f32[2,4096,512]{2,0,1:T(2,128)}, u32[]{:S(2)}, u32[]{:S(2)}) async-start(f32[2,4096,512]{2,0,1:T(2,128)} %copy.199), calls=%async_computation.4 | async-start | bytes 33554432 | tf_op jit(solution)/shard_map/all_to_all | solution.py:87
  2222.9 5.6 collective-permute-start
  2346.9 2.0 copy-start.1
  2346.9 2.0 copy-start.3
where the time goes:
time: 2410 us; the launch traced here: 2390 us
  waiting for transfers between devices  1450 us (60%)
  local copies, waits for them, and re-layouts  460 us (19%)
  matrix products  255 us (11%)
  other arithmetic  204 us (8%)
  starting transfers between devices  24.3 us (1%)
    all_to_all x2, waiting for transfers between devices, spread(): lax.all_to_all(values, ('row', 'col'), split_axis=2, concat_axis=1, tiled...  748 us
    all_to_all x2, waiting for transfers between devices, collect(): lax.all_to_all(values, ('row', 'col'), split_axis=1, concat_axis=2, tiled...  687 us
    sub x8, other arithmetic, complex_product(): real_part = values[0] * cos_part - values[1] * sin_part  128 us
    another operation x2, local copies, waits for them, and re-layouts, complex_product(): return jnp.stack([real_part, imag_part])  94 us
    dot_general x3, matrix products, dft_rows(): jnp.einsum('cbdq,ckbm->dqkm', dft_table(inner_radix, direction), partial_...  81.5 us
    dot_general x3, matrix products, dft_rows(): jnp.einsum('cadk,cabm->dkbm', dft_table(outer_radix, direction), blocked,...  75.5 us
    dot_general x2, matrix products, dft_cols(): jnp.einsum('cbdq,cmkb->dmqk', dft_table(inner_radix, direction), partial_...  63.2 us
    add x1, other arithmetic, local(): weighted + filter_taps[tap_delay][None, :, None] * turned[:, :, offset:of...  50 us
  transfers between devices with their start and end apart: 6, of which 6 were waited for; matrix products, arithmetic and copies ran while one was open for 11% of the time, Pallas kernels for 0%

commit v1 on v0

--- a/solution.py
+++ b/solution.py
@@ -84,7 +84,15 @@
 
 
 def collect(values):
-    return lax.all_to_all(values, ("row", "col"), split_axis=1, concat_axis=2, tiled=True)
+    return jnp.concatenate(
+        lax.all_to_all(
+            jnp.stack(jnp.split(values, lax.axis_size(("row", "col")), axis=1)),
+            ("row", "col"),
+            0,
+            0,
+        ),
+        axis=2,
+    )
 
 
 def local(voltage, chirp_phase, filter_taps):

time: 2410 us -> 2390 us (level)
  local copies, waits for them, and re-layouts: 460 us -> 408 us
  other arithmetic: 204 us -> 229 us
    all_to_all x3 -> x0, local copies, waits for them, and re-layouts: 49.4 us -> none  [collect(): lax.all_to_all(values, ('row', 'col'), split_axis=1, concat_axis=2, tiled...]
    another operation x2 -> x1, local copies, waits for them, and re-layouts: 94 us -> 61.7 us  [complex_product(): return jnp.stack([real_part, imag_part])]
    unnamed x12 -> x47, local copies, waits for them, and re-layouts: 34 us -> 59.7 us
    unnamed x0 -> x31, other arithmetic: none -> 25.7 us
  transfers between devices with their start and end apart: 6 -> 6, of which waited for: 6 -> 6; matrix products, arithmetic and copies ran while one was open for 11% -> 10% of each run, Pallas kernels for 0% -> 0%
where the time goes in v1:
time: 2390 us; the launch traced here: 2370 us
  waiting for transfers between devices  1460 us (61%)
  local copies, waits for them, and re-layouts  408 us (17%)
  matrix products  255 us (11%)
  other arithmetic  229 us (10%)
  starting transfers between devices  24.3 us (1%)
    all_to_all x2, waiting for transfers between devices, spread(): lax.all_to_all(values, ('row', 'col'), split_axis=2, concat_axis=1, tiled...  748 us
    all_to_all x2, waiting for transfers between devices, collect(): lax.all_to_all(jnp.stack(jnp.split(values, lax.axis_size(('row', 'col')),...  687 us
    sub x8, other arithmetic, complex_product(): real_part = values[0] * cos_part - values[1] * sin_part  128 us
    dot_general x3, matrix products, dft_rows(): jnp.einsum('cbdq,ckbm->dqkm', dft_table(inner_radix, direction), partial_...  81.5 us
    dot_general x3, matrix products, dft_rows(): jnp.einsum('cadk,cabm->dkbm', dft_table(outer_radix, direction), blocked,...  75.5 us
    dot_general x2, matrix products, dft_cols(): jnp.einsum('cbdq,cmkb->dmqk', dft_table(inner_radix, direction), partial_...  63.2 us
    another operation x1, local copies, waits for them, and re-layouts, complex_product(): return jnp.stack([real_part, imag_part])  61.7 us
    unnamed x47, local copies, waits for them, and re-layouts  59.7 us
  transfers between devices with their start and end apart: 6, of which 6 were waited for; matrix products, arithmetic and copies ran while one was open for 10% of the time, Pallas kernels for 0%

profile of v1, /device:TPU:6, one launch (start us, length us, event | category | flops | bytes accessed | tf_op | source)
XLA Modules:
  0.0 2374.4 jit_solution(6781259854117423444)
XLA Ops:
  0.0 24.9 %copy.128 = f32[2,128,16384]{1,0,2:T(2,128)} copy(f32[2,128,16384]{2,1,0:T(8,128)} %param.3) | data formatting | bytes 33554432 | tf_op args[0]
  40.1 370.0 %all-to-all-done = f32[2,128,16384]{1,0,2:T(2,128)} async-done(((f32[2,128,16384]{1,0,2:T(2,128)}), f32[2,128,16384]{1,0,2:T(2,128)}, u32[]{:S(2)}, u32[]{:S(2)}) %all-to-all-start) | async-done | bytes 16777248 | tf_op jit(solution)/shard_map/all_to_all | solution.py:83
  414.6 20.2 copy.190
  434.8 21.7 fusion.71
  466.8 28.9 %fusion.59 = f32[2,128,32,512]{3,1,2,0:T(8,128)S(1)} fusion(f32[2,32,128,512]{3,1,2,0:T(8,128)S(1)} %pad_maximum_fusion, f32[1,128,2,128]{1,3,0,2:T(8,128)S(1)} %get-tuple-element.30, f32[1,128,2,128]{1,3,0,2:T(8,128)S(1)} %get-tuple-element.29), kind=kOutput, calls=%fused_computation.163 | convolution fusion | flops 12884967424 | bytes 33816576 | tf_op jit(solution)/shard_map/cbdq,ckbm->dqkm/dot_general | solution.py:53
  519.2 36.9 %fusion.51 = (f32[1,4096,512]{2,1,0:T(8,128)S(1)}, f32[1,4096,512]{2,1,0:T(8,128)S(1)}) fusion(f32[1,128,32,512]{3,2,1,0:T(8,128)S(1)} %copy.132, f32[1,128,32,512]{3,2,1,0:T(8,128)S(1)} %copy.131, s32[512]{0:T(512)S(1)} %iota_add_fusion), kind=kLoop, calls=%fused_computation.137 | loop fusion | flops 41943040 | bytes 33556480 | tf_op jit(solution)/shard_map/sub | solution.py:28
  582.6 19.1 all-to-all-done.2
  607.9 31.5 %sine_bitcast_fusion = (f32[128,32,512]{2,0,1:T(8,128)}, f32[128,32,512]{2,0,1:T(8,128)}) fusion(f32[32,128,512]{2,1,0:T(8,128)} %all-to-all-done.2), kind=kLoop, calls=%fused_computation.153 | loop fusion | bytes 25165824 | tf_op jit(solution)/shard_map/sin | solution.py:117
  676.1 309.5 %all-to-all-done.1 = f32[32,2,128,512]{3,2,1,0:T(8,128)} async-done(((f32[32,2,128,512]{3,2,1,0:T(8,128)}), f32[32,2,128,512]{3,2,1,0:T(8,128)}, u32[]{:S(2)}, u32[]{:S(2)}) %all-to-all-start.1) | async-done | bytes 16777248 | tf_op jit(solution)/shard_map/all_to_all | solution.py:88
  985.5 17.4 copy.133
  1002.9 18.2 copy.167
  1021.1 17.1 convolution_bitcast_fusion
  1045.2 31.5 %fusion.36 = f32[2,128,128,128]{2,3,0,1:T(8,128)} fusion(f32[1,128,128,128]{2,3,0,1:T(8,128)} %get-tuple-element.14, f32[1,128,128,128]{2,3,0,1:T(8,128)} %get-tuple-element.13, f32[1,128,2,128]{1,3,0,2:T(8,128)S(1)} %copy-done.4, f32[1,128,2,128]{1,3,0,2:T(8,128)S(1)} %copy-done.1), kind=kOutput, calls=%fused_computation.119 | convolution fusion | flops 12889161728 | bytes 33816576 | tf_op jit(solution)/shard_map/cbdq,cmkb->dmqk/dot_general | solution.py:70
  1076.6 18.9 multiply_subtract_fusion.3
  1095.6 17.3 fusion.37
  1120.0 31.7 %fusion.40 = f32[2,128,128,128]{2,3,0,1:T(8,128)S(1)} fusion(f32[1,128,128,128]{2,3,0,1:T(8,128)} %get-tuple-element.12, f32[1,128,128,128]{2,3,0,1:T(8,128)} %get-tuple-element.11, f32[1,128,2,128]{1,3,2,0:T(8,128)S(1)} %get-tuple-element.28, f32[1,128,2,128]{1,3,2,0:T(8,128)S(1)} %get-tuple-element.27), kind=kOutput, calls=%fused_computation.121 | convolution fusion | flops 12889161728 | bytes 33816576 | tf_op jit(solution)/shard_map/cbdq,cmkb->dmqk/dot_general | solution.py:70
  1177.2 36.6 %fusion.49 = (f32[1,128,16384]{1,2,0:T(8,128)S(1)}, f32[1,128,16384]{1,2,0:T(8,128)S(1)}) fusion(f32[1,128,128,128]{1,3,2,0:T(8,128)} %copy.149, f32[1,128,128,128]{1,3,2,0:T(8,128)} %copy.148, s32[128]{0:T(128)S(1)} %iota_add_fusion.1), kind=kLoop, calls=%fused_computation.131 | loop fusion | flops 46137344 | bytes 33554944 | tf_op jit(solution)/shard_map/sub | solution.py:28
  1214.9 61.7 %copy.150 = f32[2,128,16384]{1,0,2:T(2,128)} copy(f32[2,128,16384]{1,2,0:T(8,128)S(1)} %pad_maximum_fusion.1) | data formatting | bytes 33554432 | tf_op jit(solution)/shard_map/stack | solution.py:30
  1281.2 377.9 %all-to-all-done.3 = f32[2,128,16384]{1,0,2:T(2,128)} async-done(((f32[2,128,16384]{1,0,2:T(2,128)}), f32[2,128,16384]{1,0,2:T(2,128)}, u32[]{:S(2)}, u32[]{:S(2)}) %all-to-all-start.3) | async-done | bytes 16777248 | tf_op jit(solution)/shard_map/all_to_all | solution.py:83
  1659.1 20.1 copy.203
  1679.2 21.7 fusion.74
  1711.1 28.9 %fusion.62 = f32[2,128,32,512]{3,1,2,0:T(8,128)S(1)} fusion(f32[2,32,128,512]{3,1,2,0:T(8,128)S(1)} %pad_maximum_fusion.2, f32[1,128,2,128]{1,3,2,0:T(8,128)S(1)} %get-tuple-element.28, f32[1,128,2,128]{1,3,2,0:T(8,128)S(1)} %get-tuple-element.27), kind=kOutput, calls=%fused_computation.164 | convolution fusion | flops 12884967424 | bytes 33816576 | tf_op jit(solution)/shard_map/cbdq,ckbm->dqkm/dot_general | solution.py:53
  1740.1 17.5 copy.155
  1788.3 377.8 %all-to-all-done.4 = f32[32,2,128,512]{3,2,1,0:T(8,128)} async-done(((f32[32,2,128,512]{3,2,1,0:T(8,128)}), f32[32,2,128,512]{3,2,1,0:T(8,128)}, u32[]{:S(2)}, u32[]{:S(2)}) %all-to-all-start.4) | async-done | bytes 16777248 | tf_op jit(solution)/shard_map/all_to_all | solution.py:88
  2166.1 17.8 copy.156
  2183.9 19.2 reshape_reshape_reshape.3
  2209.5 11.8 maximum_bitcast_fusion
  2221.3 50.0 %fusion = f32[2,1024,2048]{1,2,0:T(8,128)} fusion(f32[2,1024,2055]{1,2,0:T(8,128)} %maximum_bitcast_fusion, f32[1024]{0:T(1024)S(1)} %bitcast.459, f32[1024]{0:T(1024)S(1)} %bitcast.460, f32[1024]{0:T(1024)S(1)} %bitcast.454, f32[1024]{0:T(1024)S(1)} %bitcast.455, f32[1024]{0:T(1024)S(1)} %bitcast.456, f32[1024]{0:T(1024)S(1)} %bitcast.457, ...), kind=kLoop, calls=%fused_computation.64 | loop fusion | flops 62914560 | bytes 151027712 | tf_op jit(solution)/shard_map/add | solution.py:137
  2271.4 17.3 copy.157
  2288.7 32.0 %fusion.65 = f32[2,8,128,2048]{3,1,2,0:T(8,128)} fusion(f32[2,8,128,2048]{3,2,1,0:T(8,128)} %bitcast.449, f32[1,8,2,8]{1,3,0,2:T(8,128)S(1)} %copy.126, f32[1,8,2,8]{1,3,0,2:T(8,128)S(1)} %copy.125), kind=kOutput, calls=%fused_computation.165 | convolution fusion | flops 805306624 | bytes 33555456 | tf_op jit(solution)/shard_map/cadk,cabm->dkbm/dot_general | solution.py:48
  2330.1 23.7 fusion.68
  2353.8 20.2 copy.233
  (134 shorter events, 224.5 us)
Async XLA Ops:
  24.9 385.2 %all-to-all-start = ((f32[2,128,16384]{1,0,2:T(2,128)}), f32[2,128,16384]{1,0,2:T(2,128)}, u32[]{:S(2)}, u32[]{:S(2)}) async-start(f32[2,128,16384]{1,0,2:T(2,128)} %copy.128), calls=%async_computation | async-start | bytes 33554432 | tf_op jit(solution)/shard_map/all_to_all | solution.py:83
  410.1 191.6 %all-to-all-start.2 = ((f32[32,128,512]{2,1,0:T(8,128)}), f32[32,128,512]{2,1,0:T(8,128)}, u32[]{:S(2)}, u32[]{:S(2)}) async-start(f32[32,128,512]{2,1,0:T(8,128)} %bitcast.450), calls=%async_computation.2 | async-start | bytes 16777216 | tf_op jit(solution)/shard_map/all_to_all | solution.py:114
  414.6 52.2 %copy-start = (f32[1,128,2,128]{1,3,0,2:T(8,128)}, f32[1,128,2,128]{1,3,0,2:T(8,128)S(1)}, u32[]{:S(2)}) copy-start(f32[1,128,2,128]{1,3,0,2:T(8,128)S(1)} %get-tuple-element.29) | copy-start | bytes 393220
  414.6 52.2 %copy-start.3 = (f32[1,128,2,128]{1,3,0,2:T(8,128)}, f32[1,128,2,128]{1,3,0,2:T(8,128)S(1)}, u32[]{:S(2)}) copy-start(f32[1,128,2,128]{1,3,0,2:T(8,128)S(1)} %get-tuple-element.30) | copy-start | bytes 393220
  601.7 383.8 %all-to-all-start.1 = ((f32[32,2,128,512]{3,2,1,0:T(8,128)}), f32[32,2,128,512]{3,2,1,0:T(8,128)}, u32[]{:S(2)}, u32[]{:S(2)}) async-start(f32[32,2,128,512]{3,2,1,0:T(8,128)} %fusion.143), calls=%async_computation.1 | async-start | bytes 33554432 | tf_op jit(solution)/shard_map/all_to_all | solution.py:88
  1002.9 18.2 copy-start.1
  1002.9 18.2 copy-start.4
  1276.7 382.4 %all-to-all-start.3 = ((f32[2,128,16384]{1,0,2:T(2,128)}), f32[2,128,16384]{1,0,2:T(2,128)}, u32[]{:S(2)}, u32[]{:S(2)}) async-start(f32[2,128,16384]{1,0,2:T(2,128)} %copy.150), calls=%async_computation.3 | async-start | bytes 33554432 | tf_op jit(solution)/shard_map/all_to_all | solution.py:83
  1784.1 4.2 copy-start.6
  1784.1 382.1 %all-to-all-start.4 = ((f32[32,2,128,512]{3,2,1,0:T(8,128)}), f32[32,2,128,512]{3,2,1,0:T(8,128)}, u32[]{:S(2)}, u32[]{:S(2)}) async-start(f32[32,2,128,512]{3,2,1,0:T(8,128)} %fusion.110), calls=%async_computation.4 | async-start | bytes 33554432 | tf_op jit(solution)/shard_map/all_to_all | solution.py:88
  2204.0 5.6 collective-permute-start
  2328.0 2.0 copy-start.2
  2328.0 2.0 copy-start.5
